TPU v7x, 32 devices: a whole 2x2x4 slice. The times are simulated.
32 devices in a mesh: seq: 4 (over x, core), tensor: 8 (over z, y).
Axes of the slice: x: 2, y: 2, z: 4, core: 2. Of those that a mesh axis runs over, the one named last changes fastest.
Arguments:
- token_ids: int32 [2, 7], replicated, may hold values from 0 to 131071
- cache_lengths: int32 [7], replicated, may hold values from 1 to 5118
- embed_table: bfloat16 [131072, 1024], P('seq', 'tensor'), may hold values from -64 to 64
- attn_gain: float32 [1024], replicated, may hold values from 0.1 to 1.9
- final_gain: float32 [1024], replicated, may hold values from 0.1 to 1.9
- w_qkv: bfloat16 [1024, 3, 1024], P(None, None, 'tensor'), may hold values from -0.1875 to 0.1875
- w_out: bfloat16 [1024, 1024], P('tensor'), may hold values from -0.1875 to 0.1875
- cache_keys: bfloat16 [7, 5120, 1024], P(None, 'seq', 'tensor'), may hold values from -300 to 300
- cache_values: bfloat16 [7, 5120, 1024], P(None, 'seq', 'tensor'), may hold values from -24 to 24
Outputs:
- hidden: bfloat16 [2, 7, 1024], P(None, None, 'tensor')
- new_kv: bfloat16 [2, 2, 7, 1024], P(None, None, None, 'tensor')
- logprobs: float32 [2, 7, 131072], P(None, None, ('seq', 'tensor'))
All inputs are finite; a program needn't handle non-finite values.
Results may differ from a plain program's by a relative error of at most 0.0085.
The roundings to bfloat16 on the way count: a program that leaves them out, or rounds other values in their place, can miss the bound.
Values may be sent and summed in bfloat16 or wider, within the bound.
A program may use at most 64 MiB of HBM per device.

v0:
```python
import math

import jax
import jax.numpy as jnp
from jax import lax
from jax.sharding import PartitionSpec as P

HD = 128


epsilon = 1e-05
logit_gain = 2.0


def combined_all(value, axis, join):
    pieces = jax.tree.map(lambda part: lax.all_gather(part, axis), value)
    head = jax.tree.map(lambda part: part[0], pieces)
    tail = jax.tree.map(lambda part: part[1:], pieces)
    running, _ = lax.scan(lambda running, share: (join(running, share), None), head, tail)
    return running


def rotate(vector, positions):
    half_size = vector.shape[-1] // 2
    frequency = 10000.0 ** (-(jnp.arange(half_size, dtype=jnp.float32) * 2.0 / vector.shape[-1]))
    angles = positions.astype(jnp.float32)[..., None] * frequency
    cosine_term = jnp.cos(angles)[:, :, None, :]
    sine_term = jnp.sin(angles)[:, :, None, :]
    first_half = vector[..., :half_size]
    second_half = vector[..., half_size:]
    return jnp.concatenate(
        [
            first_half * cosine_term - second_half * sine_term,
            first_half * sine_term + second_half * cosine_term,
        ],
        -1,
    )


def pair_join(earlier, later):
    highest = jnp.maximum(earlier[0], later[0])
    return (
        highest,
        earlier[1] * jnp.exp(earlier[0] - highest) + later[1] * jnp.exp(later[0] - highest),
    )


def body(
    token_ids,
    cache_lengths,
    embed_table,
    attn_gain,
    final_gain,
    w_qkv,
    w_out,
    cache_keys,
    cache_values,
):
    streams = token_ids.shape[1]
    vocab_rows, local_width = embed_table.shape
    model_width = attn_gain.shape[0]
    heads_here = local_width // HD
    slot_count = cache_keys.shape[1]
    seq_index = lax.axis_index("seq")
    tensor_index = lax.axis_index("tensor")
    local_ids = token_ids - seq_index * vocab_rows
    inside = (local_ids >= 0) & (local_ids < vocab_rows)
    picked = embed_table[jnp.clip(local_ids, 0, vocab_rows - 1)]
    picked = jnp.where(inside[..., None], picked, jnp.zeros_like(picked))
    embed_local = lax.psum(picked.astype(jnp.float32).astype(jnp.bfloat16), "seq").astype(
        jnp.float32
    )
    embed_whole = lax.all_gather(
        embed_local.astype(jnp.bfloat16), "tensor", axis=2, tiled=True
    ).astype(jnp.float32)
    normed = (
        embed_whole
        * lax.rsqrt(jnp.mean(embed_whole * embed_whole, -1, keepdims=True) + epsilon)
        * attn_gain
    ).astype(jnp.bfloat16)
    projected = jnp.einsum("sbd,dcf->sbcf", normed, w_qkv, preferred_element_type=jnp.float32)
    head_shape = (2, streams, heads_here, HD)
    positions = cache_lengths[None, :] + jnp.arange(2, dtype=jnp.int32)[:, None]
    queries = rotate(projected[:, :, 0].reshape(head_shape), positions).astype(jnp.bfloat16)
    new_keys = rotate(projected[:, :, 1].reshape(head_shape), positions).astype(jnp.bfloat16)
    new_values = projected[:, :, 2].reshape(head_shape).astype(jnp.bfloat16)
    new_kv = jnp.stack(
        [new_keys.reshape(2, streams, local_width), new_values.reshape(2, streams, local_width)]
    )
    inverse = HD ** (-0.5)
    key_rows = cache_keys.reshape(streams, slot_count, heads_here, HD)
    value_rows = cache_values.reshape(streams, slot_count, heads_here, HD)
    scores = (
        jnp.einsum("sbhe,bjhe->sbhj", queries, key_rows, preferred_element_type=jnp.float32)
        * inverse
    )
    slot_positions = seq_index * slot_count + jnp.arange(slot_count, dtype=jnp.int32)
    visible = (slot_positions[None, :] < cache_lengths[:, None])[None, :, None, :]
    local_max = jnp.max(jnp.where(visible, scores, -1e30), -1)
    weights = jnp.where(visible, jnp.exp(scores - local_max[..., None]), 0.0)
    local_sum = jnp.sum(weights, -1)
    local_out = jnp.einsum(
        "sbhj,bjhe->sbhe",
        weights,
        value_rows,
        preferred_element_type=jnp.float32,
        precision=lax.Precision.HIGHEST,
    )
    highest = lax.pmax(local_max, "seq")
    factor = jnp.exp(local_max - highest)
    cache_total, cache_out = lax.psum((local_sum * factor, local_out * factor[..., None]), "seq")
    fresh_scores = (
        jnp.einsum("sbhe,tbhe->sbht", queries, new_keys, preferred_element_type=jnp.float32)
        * inverse
    )
    allowed = (jnp.arange(2)[None, :] <= jnp.arange(2)[:, None])[:, None, None, :]
    fresh_max = jnp.max(jnp.where(allowed, fresh_scores, -1e30), -1)
    overall = jnp.maximum(highest, fresh_max)
    fresh_weights = jnp.where(allowed, jnp.exp(fresh_scores - overall[..., None]), 0.0)
    cache_scale = jnp.exp(highest - overall)
    denominator = cache_total * cache_scale + jnp.sum(fresh_weights, -1)
    numerator = cache_out * cache_scale[..., None] + jnp.einsum(
        "sbht,tbhe->sbhe",
        fresh_weights,
        new_values,
        preferred_element_type=jnp.float32,
        precision=lax.Precision.HIGHEST,
    )
    attended = (
        (numerator / denominator[..., None]).astype(jnp.bfloat16).reshape(2 * streams, local_width)
    )
    mixed_rows = jnp.dot(attended, w_out, preferred_element_type=jnp.float32).reshape(
        2, streams, model_width
    )
    mixed_local = lax.psum_scatter(mixed_rows, "tensor", scatter_dimension=2, tiled=True)
    hidden = (embed_local + mixed_local).astype(jnp.bfloat16)
    hidden_float = hidden.astype(jnp.float32)
    final_squares = lax.psum(jnp.sum(hidden_float * hidden_float, -1), "tensor")
    factor_rows = (
        lax.rsqrt(final_squares / model_width + epsilon) * (logit_gain / math.sqrt(model_width))
    ).reshape(2 * streams, 1)
    final_local = lax.dynamic_slice_in_dim(final_gain, tensor_index * local_width, local_width)
    gated_rows = (hidden_float * final_local).astype(jnp.bfloat16).reshape(2 * streams, local_width)
    partial_logits = lax.dot_general(
        gated_rows, embed_table, (((1,), (1,)), ((), ())), preferred_element_type=jnp.float32
    )
    shares = (
        lax.psum_scatter(partial_logits, "tensor", scatter_dimension=1, tiled=True) * factor_rows
    )
    share_max = jnp.max(shares, -1)
    share_sum = jnp.sum(jnp.exp(shares - share_max[:, None]), -1)
    vocab_max, vocab_sum = combined_all((share_max, share_sum), ("seq", "tensor"), pair_join)
    logprobs = shares - (vocab_max + jnp.log(vocab_sum))[:, None]
    return (hidden, new_kv, logprobs.reshape(2, streams, -1))


def solution(mesh):
    in_specs = (
        P(),
        P(),
        P("seq", "tensor"),
        P(),
        P(),
        P(None, None, "tensor"),
        P("tensor", None),
        P(None, "seq", "tensor"),
        P(None, "seq", "tensor"),
    )
    out_specs = (
        P(None, None, "tensor"),
        P(None, None, None, "tensor"),
        P(None, None, ("seq", "tensor")),
    )
    return jax.shard_map(body, mesh=mesh, in_specs=in_specs, out_specs=out_specs, check_vma=False)
```

profile of v0, /device:TPU:0, one launch (start us, length us, event | category | flops | bytes accessed | tf_op | source)
XLA Modules:
  0.0 251.6 jit_solution(10912633208323982474)
XLA Ops:
  7.2 0.8 compare_select_fusion
  8.1 0.7 compare_and_fusion
  9.5 0.7 broadcast_compare_fusion
  10.3 5.0 %gather_fusion = bf16[14,128]{1,0:T(8,128)(2,1)S(1)} fusion(bf16[32768,128]{1,0:T(8,128)(2,1)} %param.13, s32[1024]{0:T(1024)S(1)} %pad_clamp_fusion), kind=kCustom, calls=%fused_computation | custom fusion | bytes 7224 | tf_op jit(solution)/shard_map/gather | solution.py:68
  15.4 8.3 %psum.28 = bf16[2,7,128]{2,1,0:T(8,128)(2,1)S(1)} all-reduce(bf16[2,7,128]{2,1,0:T(8,128)(2,1)S(1)} %broadcast_select_fusion), channel_id=1, replica_groups=mesh['seq'=4,'tensor'=8] {'seq'}, use_global_device_ids=true, to_apply=%region_0.1 | all-reduce | flops 1792 | bytes 7168 | tf_op jit(solution)/shard_map/psum | solution.py:70
  23.7 26.4 %all_gather.15 = bf16[2,7,1024]{2,1,0:T(8,128)(2,1)S(1)} all-gather(bf16[2,7,128]{2,1,0:T(8,128)(2,1)S(1)} %psum.28), channel_id=1, replica_groups=mesh['seq'=4,'tensor'=8] {'tensor'}, dimensions={2}, use_global_device_ids=true | all-gather | bytes 32256 | tf_op jit(solution)/shard_map/all_gather | solution.py:73
  50.2 1.4 fusion.11
  51.8 0.8 select_reduce_fusion
  53.1 5.8 %pmax.7 = f32[2,7,1]{1,0,2:T(2,128)S(1)} all-reduce(f32[2,7,1]{1,0,2:T(2,128)S(1)} %bitcast.154), channel_id=1, replica_groups=mesh['seq'=4,'tensor'=8] {'seq'}, use_global_device_ids=true, to_apply=%region_3.4 | all-reduce | flops 14 | bytes 112 | tf_op jit(solution)/shard_map/pmax | solution.py:109
  59.5 2.7 %fusion.6 = f32[2,7,1,128]{3,0,1,2:T(2,128)S(1)} fusion(bf16[7,1280,128]{2,1,0:T(8,128)(2,1)} %param.19, f32[2,7,1,1280]{3,0,1,2:T(2,128)S(1)} %get-tuple-element.74, pred[7,1280]{1,0:T(8,128)(4,1)S(1)} %broadcast_compare_fusion, f32[2,7]{0,1:T(8,128)S(1)} %get-tuple-element.73, f32[2,7]{0,1:T(8,128)S(1)} %copy.54), kind=kOutput, calls=%fused_computation.12 | convolution fusion | flops 27562752 | bytes 2381680 | tf_op jit(solution)/shard_map/sbhj,bjhe->sbhe/dot_general | solution.py:102
  62.2 5.8 %all-reduce.3 = (f32[2,7,1,128]{3,0,1,2:T(2,128)S(1)}, f32[2,7,1]{1,0,2:T(2,128)S(1)}) all-reduce(f32[2,7,1,128]{3,0,1,2:T(2,128)S(1)} %fusion.6, f32[2,7,1]{1,0,2:T(2,128)S(1)} %get-tuple-element.70), channel_id=1, replica_groups=mesh['seq'=4,'tensor'=8] {'seq'}, use_global_device_ids=true, to_apply=%region_4.5 | all-reduce | flops 1806 | bytes 14448 | tf_op jit(solution)/shard_map/psum | solution.py:111
  68.4 0.8 fusion.13
  69.3 0.8 dynamic_slice.10
  70.1 53.2 %reduce-scatter.3.cloned.1.call-done = f32[2,7,128]{2,1,0:T(8,128)} async-done(((f32[2,7,1024]{2,1,0:T(8,128)}), f32[2,7,128]{2,1,0:T(8,128)}) %reduce-scatter.3.cloned.1.call-update) | async-done | bytes 7184 | tf_op jit(solution)/shard_map/reduce_scatter | solution.py:135
  123.3 0.8 fusion.33
  124.1 7.0 %fusion.62 = f32[14,32768]{1,0:T(8,128)} fusion(bf16[14,128]{1,0:T(8,128)(2,1)S(1)} %reshape.218, bf16[32768,128]{1,0:T(8,128)(2,1)} %param.13), kind=kOutput, calls=%fused_computation.106 | convolution fusion | flops 117440512 | bytes 10227200 | tf_op jit(solution)/shard_map/dot_general | solution.py:144
  131.8 19.6 %psum.31 = f32[2,7]{1,0:T(2,128)S(1)} all-reduce(f32[2,7]{1,0:T(2,128)S(1)} %get-tuple-element.58), channel_id=1, replica_groups=mesh['seq'=4,'tensor'=8] {'tensor'}, use_global_device_ids=true, to_apply=%region_12.13 | all-reduce | flops 14 | bytes 112 | tf_op jit(solution)/shard_map/psum | solution.py:138
  152.1 46.9 %reduce-scatter.5.cloned.1.call-done = f32[14,4096]{1,0:T(8,128)} async-done(((f32[14,32768]{1,0:T(8,128)}), f32[14,4096]{1,0:T(8,128)}) %reduce-scatter.5.cloned.1.call-update) | async-done | bytes 229392 | tf_op jit(solution)/shard_map/reduce_scatter | solution.py:148
  199.0 1.2 multiply_reduce_fusion
  200.4 1.2 exponential_reduce_fusion
  201.9 39.3 %all-reduce.2 = (f32[448]{0:T(512)S(1)}, f32[448]{0:T(512)S(1)}) all-reduce(f32[448]{0:T(512)S(1)} %dynamic-update-slice, f32[448]{0:T(512)S(1)} %dynamic-update-slice.1), channel_id=2, replica_groups=mesh['seq'=4,'tensor'=8] {'seq','tensor'}, use_global_device_ids=true, to_apply=%add | all-reduce | flops 896 | bytes 7168
  241.6 1.2 while.12
  242.8 1.0 multiply_subtract_fusion
  243.9 0.9 copy.69
  (85 shorter events, 5.7 us)
Async XLA Ops:
  7.2 44.7 %copy-start = (bf16[7,1280,128]{2,1,0:T(8,128)(2,1)S(1)}, bf16[7,1280,128]{2,1,0:T(8,128)(2,1)}, u32[]{:S(2)}) copy-start(bf16[7,1280,128]{2,1,0:T(8,128)(2,1)} %param.18) | copy-start | bytes 6881284
  7.2 116.1 %reduce-scatter.3.cloned.1.call-start = ((), (), s32[]{:S(2)}) async-start(), calls=%async_computation.2 | async-start | bytes 73728 | tf_op jit(solution)/shard_map/reduce_scatter | solution.py:135
  51.8 16.6 %copy-start.1 = (bf16[128,1024]{1,0:T(8,128)(2,1)S(1)}, bf16[128,1024]{1,0:T(8,128)(2,1)}, u32[]{:S(2)}) copy-start(bf16[128,1024]{1,0:T(8,128)(2,1)} %param.17) | copy-start | bytes 786436
  69.3 129.8 %reduce-scatter.5.cloned.1.call-start = ((), (), s32[]{:S(2)}) async-start(), calls=%async_computation.3 | async-start | bytes 2359296 | tf_op jit(solution)/shard_map/reduce_scatter | solution.py:148
Sparse Core Ops, SparseCore 0:
  69.4 53.8 reduce-scatter.2
  131.3 67.7 reduce-scatter.4
where the time goes:
time: 252 us
  blocking collectives  105 us (42%)
  waiting for transfers between devices  100 us (40%)
  between operations  14.2 us (6%)
  matrix products  13 us (5%)
  local copies, waits for them, and re-layouts  9.57 us (4%)
  other arithmetic  8.84 us (4%)
    reduce_scatter x1, waiting for transfers between devices, body(): lax.psum_scatter(mixed_rows, 'tensor', scatter_dimension=2, tiled=True)  53.2 us
    reduce_scatter x1, waiting for transfers between devices, body(): lax.psum_scatter(partial_logits, 'tensor', scatter_dimension=1, tiled=True)  46.9 us
    unnamed x1, blocking collectives  39.3 us
    all_gather x1, blocking collectives, body(): lax.all_gather(embed_local.astype(jnp.bfloat16), 'tensor', axis=2, tiled=...  26.4 us
    psum x1, blocking collectives, body(): final_squares = lax.psum(jnp.sum(hidden_float * hidden_float, -1), 'tensor')  19.6 us
    psum x1, blocking collectives, body(): lax.psum(picked.astype(jnp.float32).astype(jnp.bfloat16), 'seq')  8.35 us
    dot_general x1, matrix products, body(): lax.dot_general(gated_rows, embed_table, (((1,), (1,)), ((), ())), prefer...  7.03 us
    pmax x1, blocking collectives, body(): highest = lax.pmax(local_max, 'seq')  5.85 us
  transfers between devices with their start and end apart: 2, of which 2 were waited for; matrix products, arithmetic and copies ran while one was open for 1% of the time, Pallas kernels for 0%

commit v1 on v0

v1 whole, which is shorter than its diff:
```python
import functools
import math

import numpy as np

import jax
import jax.numpy as jnp
from jax import lax
from jax.experimental import pallas as pl
from jax.experimental.pallas import tpu as pltpu
from jax.sharding import PartitionSpec as P

HD = 128
ROWS = 16
TILE = 16
BF = jnp.bfloat16
F32 = jnp.float32

epsilon = 1e-05
logit_gain = 2.0


def nt_dot(a, b):
    return lax.dot_general(a, b, (((1,), (1,)), ((), ())), preferred_element_type=F32)


def local_kernel(streams, tok_ref, len_ref, freq_ref, table_hbm, pick_ref, lens_ref, cos_ref, sin_ref, blocks, sem):
    first = lax.axis_index("seq") * table_hbm.shape[0]
    last = table_hbm.shape[0] - 1
    lines = []
    copies = []
    for b in range(streams):
        for s in range(2):
            at = tok_ref[s, b] - first
            inside = (at >= 0) & (at <= last)
            safe = jnp.clip(at, 0, last)
            base = lax.div(safe, TILE) * TILE
            copy = pltpu.make_async_copy(
                table_hbm.at[pl.ds(pl.multiple_of(base, TILE), TILE)],
                blocks.at[2 * b + s],
                sem.at[2 * b + s],
            )
            copy.start()
            copies.append(copy)
            lines.append(jnp.where(inside, safe - base, -1))
    row = lax.broadcasted_iota(jnp.int32, (ROWS, HD), 0)
    lane = lax.broadcasted_iota(jnp.int32, (ROWS, HD), 1)
    lens = jnp.ones((ROWS, HD), jnp.int32)
    for b in range(streams):
        lens = jnp.where(lax.div(row, 2) == b, len_ref[b], lens)
    lens_ref[...] = lens
    angle = (lens + lax.rem(row, 2)).astype(F32) * freq_ref[...]
    cos_ref[...] = jnp.cos(angle)
    sine = jnp.sin(angle)
    sin_ref[...] = jnp.where(lane < HD // 2, -sine, sine)
    picked = jnp.zeros((ROWS, HD), F32)
    for i in range(2 * streams):
        copies[i].wait()
        line = jnp.where(row == lines[i], blocks[i].astype(F32), 0.0)
        picked = jnp.where(row == i, jnp.sum(line, 0, keepdims=True), picked)
    pick_ref[...] = picked.astype(BF)


def kernel(
    n_seq, n_tensor, streams, model_width,
    pick_ref, lens_ref, cos_ref, sin_ref, again_ref, fgain_ref, table_hbm, wqkv_hbm, wout_hbm, keys_hbm, values_hbm,
    hidden_ref, newkv_ref, logp_ref,
    table, wqkv, wout, keys, values,
    pick_all, emb_all, flash_all, mix_out, mix_all, sq_all, lsa_all, lsb_all,
    pair_out, pair_in, own, far_out, far_in, logits,
    dma_sem,
    pick_s, pick_r, emb_s, emb_r, flash_s, flash_r, mix_s, mix_r, sq_s, sq_r,
    lsa_s, lsa_r, lsb_s, lsb_r, pair_s, pair_r, far_s, far_r,
):
    me_s = lax.axis_index("seq")
    me_t = lax.axis_index("tensor")
    vocab_rows = table.shape[0]
    slot_count = keys.shape[1]
    groups = n_tensor // 2
    share = vocab_rows // n_tensor

    parts = 4
    piece = vocab_rows // parts
    loads = [
        pltpu.make_async_copy(
            table_hbm.at[pl.ds(i * piece, piece)], table.at[pl.ds(i * piece, piece)], dma_sem.at[i]
        )
        for i in range(parts)
    ]
    load_wqkv = pltpu.make_async_copy(wqkv_hbm, wqkv, dma_sem.at[parts])
    load_keys = pltpu.make_async_copy(keys_hbm, keys, dma_sem.at[parts + 1])
    load_values = pltpu.make_async_copy(values_hbm, values, dma_sem.at[parts + 2])
    load_wout = pltpu.make_async_copy(wout_hbm, wout, dma_sem.at[parts + 3])
    for load in loads + [load_wqkv, load_keys, load_values, load_wout]:
        load.start()

    def seq_peer(k):
        return lax.rem(me_s + k, n_seq)

    def tensor_peer(k):
        return lax.rem(me_t + k, n_tensor)

    barrier = pltpu.get_barrier_semaphore()
    for k in range(1, n_seq):
        pl.semaphore_signal(
            barrier, inc=1, device_id=(seq_peer(k), me_t), device_id_type=pl.DeviceIdType.MESH
        )
    for k in range(1, n_tensor):
        pl.semaphore_signal(
            barrier, inc=1, device_id=(me_s, tensor_peer(k)), device_id_type=pl.DeviceIdType.MESH
        )

    def exchange(src_of, dst, send, recv, axis):
        count = n_seq if axis == "seq" else n_tensor
        mine = me_s if axis == "seq" else me_t
        copies = []
        for k in range(1, count):
            if axis == "seq":
                peer = seq_peer(k)
                target = (peer, me_t)
            else:
                peer = tensor_peer(k)
                target = (me_s, peer)
            copy = pltpu.make_async_remote_copy(
                src_ref=src_of(peer),
                dst_ref=dst.at[mine],
                send_sem=send.at[k],
                recv_sem=recv.at[k],
                device_id=target,
                device_id_type=pl.DeviceIdType.MESH,
            )
            copy.start()
            copies.append(copy)
        return copies

    row = lax.broadcasted_iota(jnp.int32, (ROWS, HD), 0)
    lane = lax.broadcasted_iota(jnp.int32, (ROWS, HD), 1)
    stream = lax.div(row, 2)
    step = lax.rem(row, 2)
    lens = lens_ref[...]
    cosine = cos_ref[...]
    sine = sin_ref[...]
    pick_all[me_s] = pick_ref[...]
    pl.semaphore_wait(barrier, n_seq - 1 + n_tensor - 1)
    sent = exchange(lambda peer: pick_ref, pick_all, pick_s, pick_r, "seq")
    for copy in sent:
        copy.wait_recv()
    embed = pick_all[0].astype(F32)
    for i in range(1, n_seq):
        embed = embed + pick_all[i].astype(F32)
    emb_all[me_t] = embed.astype(BF)
    more = exchange(lambda peer: emb_all.at[me_t], emb_all, emb_s, emb_r, "tensor")
    load_wqkv.wait()
    for load in loads:
        load.wait()
    for copy in more:
        copy.wait_recv()
    sent += more
    squares = jnp.zeros((ROWS, HD), F32)
    for i in range(n_tensor):
        part = emb_all[i].astype(F32)
        squares = squares + part * part
    norm = lax.rsqrt(jnp.sum(squares, -1, keepdims=True) / model_width + epsilon)
    normed = jnp.concatenate(
        [
            (emb_all[i].astype(F32) * norm * again_ref[:, i * HD : (i + 1) * HD]).astype(BF)
            for i in range(n_tensor)
        ],
        1,
    )
    projected = [jnp.dot(normed, wqkv[c], preferred_element_type=F32) for c in range(3)]

    def rotate(x):
        return x * cosine + pltpu.roll(x, HD // 2, 1) * sine

    queries = rotate(projected[0]).astype(BF)
    new_keys = rotate(projected[1]).astype(BF)
    new_values = projected[2].astype(BF)
    for b in range(streams):
        newkv_ref[0, b] = new_keys[2 * b : 2 * b + 2]
        newkv_ref[1, b] = new_values[2 * b : 2 * b + 2]

    inverse = HD ** (-0.5)
    load_keys.wait()
    wide_stream = lax.div(lax.broadcasted_iota(jnp.int32, (ROWS, slot_count), 0), 2)
    scores = jnp.zeros((ROWS, slot_count), F32)
    for b in range(streams):
        scores = jnp.where(wide_stream == b, nt_dot(queries, keys[b]), scores)
    scores = scores * inverse
    slot = me_s * slot_count + lax.broadcasted_iota(jnp.int32, (ROWS, slot_count), 1)
    visible = slot < lens[:, :1]
    top = jnp.max(jnp.where(visible, scores, -1e30), -1, keepdims=True)
    weights = jnp.where(visible, jnp.exp(scores - top), 0.0)
    total = jnp.sum(weights, -1, keepdims=True)
    high = weights.astype(BF)
    low = (weights - high.astype(F32)).astype(BF)
    both = jnp.concatenate([high, low], 0)
    load_values.wait()
    gathered = jnp.zeros((ROWS, HD), F32)
    for b in range(streams):
        twin = jnp.dot(both, values[b], preferred_element_type=F32)
        gathered = jnp.where(stream == b, twin[:ROWS] + twin[ROWS:], gathered)
    flash_all[me_s, :, :HD] = gathered
    flash_all[me_s, :, HD:] = jnp.where(lane < HD // 2, top, total)
    more = exchange(lambda peer: flash_all.at[me_s], flash_all, flash_s, flash_r, "seq")

    def twice(x, s):
        return jnp.where(step == s, x, pltpu.roll(x, 1 if s == 0 else ROWS - 1, 0))

    qf = queries.astype(F32)
    kf = new_keys.astype(F32)
    vf = new_values.astype(F32)
    fresh0 = jnp.sum(qf * twice(kf, 0), -1, keepdims=True) * inverse
    fresh1 = jnp.sum(qf * twice(kf, 1), -1, keepdims=True) * inverse
    second = step[:, :1] == 1
    fresh1 = jnp.where(second, fresh1, -1e30)
    fresh_top = jnp.maximum(fresh0, fresh1)
    for copy in more:
        copy.wait_recv()
    sent += more
    tops = [flash_all[i, :, HD : HD + 1] for i in range(n_seq)]
    best = fresh_top
    for item in tops:
        best = jnp.maximum(best, item)
    w0 = jnp.exp(fresh0 - best)
    w1 = jnp.where(second, jnp.exp(fresh1 - best), 0.0)
    numerator = w0 * twice(vf, 0) + w1 * twice(vf, 1)
    denominator = w0 + w1
    for i in range(n_seq):
        factor = jnp.exp(tops[i] - best)
        numerator = numerator + flash_all[i, :, :HD] * factor
        denominator = denominator + flash_all[i, :, 2 * HD - 1 : 2 * HD] * factor
    attended = (numerator / denominator).astype(BF)

    load_wout.wait()
    for i in range(n_tensor):
        mix_out[i] = jnp.dot(
            attended, wout[:, i * HD : (i + 1) * HD], preferred_element_type=F32
        )
    more = exchange(lambda peer: mix_out.at[peer], mix_all, mix_s, mix_r, "tensor")
    mix_all[me_t] = mix_out[me_t]
    for copy in more:
        copy.wait_recv()
    sent += more
    mixed = mix_all[0]
    for i in range(1, n_tensor):
        mixed = mixed + mix_all[i]
    hidden = (emb_all[me_t].astype(F32) + mixed).astype(BF)
    for b in range(streams):
        hidden_ref[b] = hidden[2 * b : 2 * b + 2]
    hf = hidden.astype(F32)
    diagonal = row == lane

    def to_lanes(column):
        return jnp.sum(jnp.where(diagonal, column, 0.0), 0, keepdims=True)

    def to_rows(line, shift):
        return jnp.sum(jnp.where(lane == row + shift, line, 0.0), -1, keepdims=True)

    gated = (hf * fgain_ref[me_t]).astype(BF)

    pair = lax.rem(me_t, 2)
    group = lax.div(me_t, 2)
    partner = me_t + 1 - 2 * pair

    def part_logits(owner):
        return nt_dot(gated, table[pl.ds(pl.multiple_of(owner * share, share), share), :])

    pair_copies = []
    for k in range(1, groups + 1):
        g = lax.rem(group + k, groups)
        pair_out[k - 1] = part_logits(2 * g + 1 - pair).astype(BF)
        copy = pltpu.make_async_remote_copy(
            src_ref=pair_out.at[k - 1],
            dst_ref=pair_in.at[k - 1],
            send_sem=pair_s.at[k - 1],
            recv_sem=pair_r.at[k - 1],
            device_id=(me_s, partner),
            device_id_type=pl.DeviceIdType.MESH,
        )
        copy.start()
        pair_copies.append(copy)
    sq_all[me_t] = to_lanes(jnp.sum(hf * hf, -1, keepdims=True))
    sq_copies = exchange(lambda peer: sq_all.at[me_t], sq_all, sq_s, sq_r, "tensor")
    for k in range(1, groups + 1):
        g = lax.rem(group + k, groups)
        own[k - 1] = part_logits(2 * g + pair)
    far_copies = []
    for k in range(1, groups):
        g = lax.rem(group + k, groups)
        pair_copies[k - 1].wait_recv()
        far_out[k - 1] = (own[k - 1] + pair_in[k - 1].astype(F32)).astype(BF)
        copy = pltpu.make_async_remote_copy(
            src_ref=far_out.at[k - 1],
            dst_ref=far_in.at[k - 1],
            send_sem=far_s.at[k - 1],
            recv_sem=far_r.at[k - 1],
            device_id=(me_s, 2 * g + pair),
            device_id_type=pl.DeviceIdType.MESH,
        )
        copy.start()
        far_copies.append(copy)
    for copy in sq_copies:
        copy.wait_recv()
    all_squares = sq_all[0]
    for i in range(1, n_tensor):
        all_squares = all_squares + sq_all[i]
    scale = lax.rsqrt(to_rows(all_squares, 0) / model_width + epsilon) * (
        logit_gain / math.sqrt(model_width)
    )
    pair_copies[groups - 1].wait_recv()
    value = own[groups - 1] + pair_in[groups - 1].astype(F32)
    for k in range(1, groups):
        far_copies[k - 1].wait_recv()
        value = value + far_in[k - 1].astype(F32)
    value = value * scale
    logits[...] = value
    high_here = jnp.max(value, -1, keepdims=True)
    sum_here = jnp.sum(jnp.exp(value - high_here), -1, keepdims=True)

    def packed(top_column, sum_column):
        return jnp.sum(
            jnp.where(diagonal, top_column, jnp.where(lane == row + ROWS, sum_column, 0.0)),
            0,
            keepdims=True,
        )

    def joined(store, count):
        highs = [to_rows(store[i], 0) for i in range(count)]
        sums = [to_rows(store[i], ROWS) for i in range(count)]
        peak = highs[0]
        for item in highs[1:]:
            peak = jnp.maximum(peak, item)
        summed = sums[0] * jnp.exp(highs[0] - peak)
        for i in range(1, count):
            summed = summed + sums[i] * jnp.exp(highs[i] - peak)
        return peak, summed

    lsa_all[me_s] = packed(high_here, sum_here)
    more = exchange(lambda peer: lsa_all.at[me_s], lsa_all, lsa_s, lsa_r, "seq")
    for copy in more:
        copy.wait_recv()
    sent += more
    lsb_all[me_t] = packed(*joined(lsa_all, n_seq))
    more = exchange(lambda peer: lsb_all.at[me_t], lsb_all, lsb_s, lsb_r, "tensor")
    for copy in more:
        copy.wait_recv()
    sent += more
    peak, summed = joined(lsb_all, n_tensor)
    answer = logits[...] - (peak + jnp.log(summed))
    for b in range(streams):
        logp_ref[b] = answer[2 * b : 2 * b + 2]
    for copy in sent + pair_copies + sq_copies + far_copies:
        copy.wait_send()


def body(
    n_seq, n_tensor,
    token_ids, cache_lengths, embed_table, attn_gain, final_gain, w_qkv, w_out, cache_keys, cache_values,
):
    streams = token_ids.shape[1]
    vocab_rows, width = embed_table.shape
    model_width = attn_gain.shape[0]
    share = vocab_rows // n_tensor
    groups = n_tensor // 2
    slot_count = cache_keys.shape[1]
    assert width == HD and 2 * streams <= ROWS and n_tensor % 2 == 0
    half = HD // 2
    powers = 10000.0 ** (-(np.arange(half, dtype=np.float64) * 2.0 / HD))
    freq = jnp.asarray(np.concatenate([powers, powers])[None].astype(np.float32))
    vmem = pl.BlockSpec(memory_space=pltpu.VMEM)
    smem = pl.BlockSpec(memory_space=pltpu.SMEM)
    hbm = pl.BlockSpec(memory_space=pl.ANY)
    sems = lambda n: pltpu.SemaphoreType.DMA((n,))
    row_shape = lambda dtype: jax.ShapeDtypeStruct((ROWS, HD), dtype)
    picked, lens, cosine, sine = pl.pallas_call(
        functools.partial(local_kernel, streams),
        out_shape=(row_shape(BF), row_shape(jnp.int32), row_shape(F32), row_shape(F32)),
        in_specs=[smem, smem, vmem, hbm],
        out_specs=(vmem,) * 4,
        scratch_shapes=[pltpu.VMEM((2 * streams, TILE, HD), BF), sems(2 * streams)],
        compiler_params=pltpu.CompilerParams(vmem_limit_bytes=60 * 1024 * 1024),
        name="rows",
    )(token_ids, cache_lengths, freq, embed_table)
    hidden, new_kv, logprobs = pl.pallas_call(
        functools.partial(kernel, n_seq, n_tensor, streams, model_width),
        out_shape=(
            jax.ShapeDtypeStruct((streams, 2, HD), BF),
            jax.ShapeDtypeStruct((2, streams, 2, HD), BF),
            jax.ShapeDtypeStruct((streams, 2, share), F32),
        ),
        in_specs=[vmem] * 6 + [hbm] * 5,
        out_specs=(vmem, vmem, vmem),
        scratch_shapes=[
            pltpu.VMEM((vocab_rows, HD), BF),
            pltpu.VMEM((3, model_width, HD), BF),
            pltpu.VMEM((HD, model_width), BF),
            pltpu.VMEM((streams, slot_count, HD), BF),
            pltpu.VMEM((streams, slot_count, HD), BF),
            pltpu.VMEM((n_seq, ROWS, HD), BF),
            pltpu.VMEM((n_tensor, ROWS, HD), BF),
            pltpu.VMEM((n_seq, ROWS, 2 * HD), F32),
            pltpu.VMEM((n_tensor, ROWS, HD), F32),
            pltpu.VMEM((n_tensor, ROWS, HD), F32),
            pltpu.VMEM((n_tensor, 1, HD), F32),
            pltpu.VMEM((n_seq, 1, HD), F32),
            pltpu.VMEM((n_tensor, 1, HD), F32),
            pltpu.VMEM((groups, ROWS, share), BF),
            pltpu.VMEM((groups, ROWS, share), BF),
            pltpu.VMEM((groups, ROWS, share), F32),
            pltpu.VMEM((groups, ROWS, share), BF),
            pltpu.VMEM((groups, ROWS, share), BF),
            pltpu.VMEM((ROWS, share), F32),
            sems(8),
            sems(n_seq), sems(n_seq), sems(n_tensor), sems(n_tensor),
            sems(n_seq), sems(n_seq), sems(n_tensor), sems(n_tensor),
            sems(n_tensor), sems(n_tensor),
            sems(n_seq), sems(n_seq), sems(n_tensor), sems(n_tensor),
            sems(groups), sems(groups), sems(groups), sems(groups),
        ],
        compiler_params=pltpu.CompilerParams(
            collective_id=0, has_side_effects=True, vmem_limit_bytes=60 * 1024 * 1024
        ),
        name="decode",
    )(
        picked,
        lens,
        cosine,
        sine,
        attn_gain.reshape(1, model_width),
        final_gain.reshape(n_tensor, 1, HD),
        embed_table,
        jnp.transpose(w_qkv, (1, 0, 2)),
        w_out,
        cache_keys,
        cache_values,
    )
    return (
        jnp.transpose(hidden, (1, 0, 2)),
        jnp.transpose(new_kv, (0, 2, 1, 3)),
        jnp.transpose(logprobs, (1, 0, 2)),
    )


def solution(mesh):
    in_specs = (
        P(),
        P(),
        P("seq", "tensor"),
        P(),
        P(),
        P(None, None, "tensor"),
        P("tensor", None),
        P(None, "seq", "tensor"),
        P(None, "seq", "tensor"),
    )
    out_specs = (
        P(None, None, "tensor"),
        P(None, None, None, "tensor"),
        P(None, None, ("seq", "tensor")),
    )
    return jax.shard_map(
        functools.partial(body, mesh.shape["seq"], mesh.shape["tensor"]),
        mesh=mesh, in_specs=in_specs, out_specs=out_specs, check_vma=False,
    )
```

time: 252 us -> 57 us (0.23)
  blocking collectives: 105 us -> 0 us
  waiting for transfers between devices: 100 us -> 0 us
  Pallas kernels: 0 us -> 51.8 us
  between operations: 14.2 us -> 0.65 us
  matrix products: 13 us -> 0 us
  other arithmetic: 8.84 us -> 0 us
  local copies, waits for them, and re-layouts: 9.57 us -> 4.2 us
    reduce_scatter x2 -> x0, waiting for transfers between devices: 100 us -> none  [the longest x1 53.2 us: body(): lax.psum_scatter(mixed_rows, 'tensor', scatter_dimension=2, tiled=True)]
    pallas_call x0 -> x2, Pallas kernels: none -> 51.8 us  [the longest x1 49.3 us: body(): pl.pallas_call(functools.partial(kernel, n_seq, n_tensor, streams, model_...]
    unnamed x1 -> x0, blocking collectives: 39.3 us -> none
    psum x3 -> x0, blocking collectives: 33.8 us -> none  [the longest x1 19.6 us: body(): final_squares = lax.psum(jnp.sum(hidden_float * hidden_float, -1), 'tensor')]
    all_gather x1 -> x0, blocking collectives: 26.4 us -> none  [body(): lax.all_gather(embed_local.astype(jnp.bfloat16), 'tensor', axis=2, tiled=...]
    dot_general x7 -> x0, matrix products: 13 us -> none  [the longest x1 7.03 us: body(): lax.dot_general(gated_rows, embed_table, (((1,), (1,)), ((), ())), prefer...]
    pmax x1 -> x0, blocking collectives: 5.85 us -> none  [body(): highest = lax.pmax(local_max, 'seq')]
    gather x2 -> x0, local copies, waits for them, and re-layouts: 5.03 us -> none  [body(): picked = embed_table[jnp.clip(local_ids, 0, vocab_rows - 1)]]
  transfers between devices with their start and end apart: 2 -> 0, of which waited for: 2 -> 0; matrix products, arithmetic and copies ran while one was open for 1% -> 0% of each run, Pallas kernels for 0% -> 0%
where the time goes in v1:
time: 57 us; the launch traced here: 56.7 us
  Pallas kernels  51.8 us (91%)
  local copies, waits for them, and re-layouts  4.2 us (7%)
  between operations  0.65 us (1%)
    pallas_call x1, Pallas kernels, body(): pl.pallas_call(functools.partial(kernel, n_seq, n_tensor, streams, model_...  49.3 us
    unnamed x3, local copies, waits for them, and re-layouts  4.2 us
    pallas_call x1, Pallas kernels, body(): pl.pallas_call(functools.partial(local_kernel, streams), out_shape=(row_s...  2.53 us

profile of v1, /device:TPU:0, one launch (start us, length us, event | category | flops | bytes accessed | tf_op | source)
XLA Modules:
  0.0 56.7 jit_solution(3396763067615130788)
XLA Ops:
  0.6 2.5 %rows.1 = (bf16[16,128]{1,0:T(8,128)(2,1)}, s32[16,128]{1,0:T(8,128)}, f32[16,128]{1,0:T(8,128)}, f32[16,128]{1,0:T(8,128)}) custom-call(s32[2,7]{1,0:T(2,128)} %tok_ref.1, s32[7]{0:T(128)} %len_ref.1, f32[1,128]{1,0:T(1,128)} %constant.2.clone.freq_ref, bf16[32768,128]{1,0:T(8,128)(2,1)} %table_hbm.3), custom_call_target="tpu_custom_call" | custom-call | tf_op jit(solution)/shard_map/rows/pallas_call | solution.py:376
  3.2 49.3 %decode.1 = (bf16[7,2,128]{2,1,0:T(2,128)(2,1)}, bf16[2,7,2,128]{3,2,1,0:T(2,128)(2,1)}, f32[7,2,4096]{2,1,0:T(2,128)}) custom-call(bf16[16,128]{1,0:T(8,128)(2,1)} %get-tuple-element.10.pick_ref, s32[16,128]{1,0:T(8,128)} %get-tuple-element.11.lens_ref, f32[16,128]{1,0:T(8,128)} %get-tuple-element.12.cos_ref, f32[16,128]{1,0:T(8,128)} %get-tuple-element.13.sin_ref, ...), custom_call_target="tpu_custom_call" | custom-call | tf_op jit(solution)/shard_map/decode/pallas_call | solution.py:385
  52.5 1.3 %copy.16 = bf16[2,7,128]{2,0,1:T(2,128)(2,1)} copy(bf16[2,7,128]{2,0,1:T(2,128)(2,1)} %bitcast.11) | data formatting | bytes 7168
  53.8 1.3 %copy.17 = bf16[2,2,7,128]{3,1,2,0:T(2,128)(2,1)} copy(bf16[2,2,7,128]{3,1,2,0:T(2,128)(2,1)} %bitcast.8) | data formatting | bytes 14336
  55.0 1.6 %copy.18 = f32[2,7,4096]{2,0,1:T(2,128)} copy(f32[2,7,4096]{2,0,1:T(2,128)} %bitcast.7) | data formatting | bytes 458752

commit v2 on v1

--- a/solution.py
+++ b/solution.py
@@ -13,6 +13,7 @@
 HD = 128
 ROWS = 16
 TILE = 16
+HALVES = 2
 BF = jnp.bfloat16
 F32 = jnp.float32
 
@@ -64,13 +65,13 @@
 def kernel(
     n_seq, n_tensor, streams, model_width,
     pick_ref, lens_ref, cos_ref, sin_ref, again_ref, fgain_ref, table_hbm, wqkv_hbm, wout_hbm, keys_hbm, values_hbm,
-    hidden_ref, newkv_ref, logp_ref,
+    hidden_ref, fresh_k_ref, fresh_v_ref, lse_ref, logits_hbm,
     table, wqkv, wout, keys, values,
-    pick_all, emb_all, flash_all, mix_out, mix_all, sq_all, lsa_all, lsb_all,
+    pick_all, emb_all, flash_all, mix_out, mix_all, sq_all, ls_all,
     pair_out, pair_in, own, far_out, far_in, logits,
     dma_sem,
     pick_s, pick_r, emb_s, emb_r, flash_s, flash_r, mix_s, mix_r, sq_s, sq_r,
-    lsa_s, lsa_r, lsb_s, lsb_r, pair_s, pair_r, far_s, far_r,
+    ls_s, ls_r, pair_s, pair_r, far_s, far_r,
 ):
     me_s = lax.axis_index("seq")
     me_t = lax.axis_index("tensor")
@@ -176,9 +177,8 @@
     queries = rotate(projected[0]).astype(BF)
     new_keys = rotate(projected[1]).astype(BF)
     new_values = projected[2].astype(BF)
-    for b in range(streams):
-        newkv_ref[0, b] = new_keys[2 * b : 2 * b + 2]
-        newkv_ref[1, b] = new_values[2 * b : 2 * b + 2]
+    fresh_k_ref[...] = new_keys
+    fresh_v_ref[...] = new_values
 
     inverse = HD ** (-0.5)
     load_keys.wait()
@@ -246,8 +246,7 @@
     for i in range(1, n_tensor):
         mixed = mixed + mix_all[i]
     hidden = (emb_all[me_t].astype(F32) + mixed).astype(BF)
-    for b in range(streams):
-        hidden_ref[b] = hidden[2 * b : 2 * b + 2]
+    hidden_ref[...] = hidden
     hf = hidden.astype(F32)
     diagonal = row == lane
 
@@ -263,43 +262,55 @@
     group = lax.div(me_t, 2)
     partner = me_t + 1 - 2 * pair
 
-    def part_logits(owner):
-        return nt_dot(gated, table[pl.ds(pl.multiple_of(owner * share, share), share), :])
+    half = share // HALVES
+
+    def part_logits(owner, h):
+        start = pl.multiple_of(owner * share + h * half, half)
+        return nt_dot(gated, table[pl.ds(start, half), :])
 
     pair_copies = []
     for k in range(1, groups + 1):
         g = lax.rem(group + k, groups)
-        pair_out[k - 1] = part_logits(2 * g + 1 - pair).astype(BF)
-        copy = pltpu.make_async_remote_copy(
-            src_ref=pair_out.at[k - 1],
-            dst_ref=pair_in.at[k - 1],
-            send_sem=pair_s.at[k - 1],
-            recv_sem=pair_r.at[k - 1],
-            device_id=(me_s, partner),
-            device_id_type=pl.DeviceIdType.MESH,
-        )
-        copy.start()
-        pair_copies.append(copy)
+        for h in range(HALVES):
+            i = (k - 1) * HALVES + h
+            pair_out[i] = part_logits(2 * g + 1 - pair, h).astype(BF)
+            copy = pltpu.make_async_remote_copy(
+                src_ref=pair_out.at[i],
+                dst_ref=pair_in.at[i],
+                send_sem=pair_s.at[i],
+                recv_sem=pair_r.at[i],
+                device_id=(me_s, partner),
+                device_id_type=pl.DeviceIdType.MESH,
+            )
+            copy.start()
+            pair_copies.append(copy)
     sq_all[me_t] = to_lanes(jnp.sum(hf * hf, -1, keepdims=True))
     sq_copies = exchange(lambda peer: sq_all.at[me_t], sq_all, sq_s, sq_r, "tensor")
+    far_copies = []
+
+    def send_far(k, h):
+        g = lax.rem(group + k, groups)
+        i = (k - 1) * HALVES + h
+        pair_copies[i].wait_recv()
+        far_out[i] = (own[i] + pair_in[i].astype(F32)).astype(BF)
+        copy = pltpu.make_async_remote_copy(
+            src_ref=far_out.at[i],
+            dst_ref=far_in.at[i],
+            send_sem=far_s.at[i],
+            recv_sem=far_r.at[i],
+            device_id=(me_s, 2 * g + pair),
+            device_id_type=pl.DeviceIdType.MESH,
+        )
+        copy.start()
+        far_copies.append(copy)
+
     for k in range(1, groups + 1):
         g = lax.rem(group + k, groups)
-        own[k - 1] = part_logits(2 * g + pair)
-    far_copies = []
+        for h in range(HALVES):
+            own[(k - 1) * HALVES + h] = part_logits(2 * g + pair, h)
     for k in range(1, groups):
-        g = lax.rem(group + k, groups)
-        pair_copies[k - 1].wait_recv()
-        far_out[k - 1] = (own[k - 1] + pair_in[k - 1].astype(F32)).astype(BF)
-        copy = pltpu.make_async_remote_copy(
-            src_ref=far_out.at[k - 1],
-            dst_ref=far_in.at[k - 1],
-            send_sem=far_s.at[k - 1],
-            recv_sem=far_r.at[k - 1],
-            device_id=(me_s, 2 * g + pair),
-            device_id_type=pl.DeviceIdType.MESH,
-        )
-        copy.start()
-        far_copies.append(copy)
+        for h in range(HALVES):
+            send_far(k, h)
     for copy in sq_copies:
         copy.wait_recv()
     all_squares = sq_all[0]
@@ -308,50 +319,80 @@
     scale = lax.rsqrt(to_rows(all_squares, 0) / model_width + epsilon) * (
         logit_gain / math.sqrt(model_width)
     )
-    pair_copies[groups - 1].wait_recv()
-    value = own[groups - 1] + pair_in[groups - 1].astype(F32)
-    for k in range(1, groups):
-        far_copies[k - 1].wait_recv()
-        value = value + far_in[k - 1].astype(F32)
-    value = value * scale
-    logits[...] = value
-    high_here = jnp.max(value, -1, keepdims=True)
-    sum_here = jnp.sum(jnp.exp(value - high_here), -1, keepdims=True)
-
-    def packed(top_column, sum_column):
-        return jnp.sum(
-            jnp.where(diagonal, top_column, jnp.where(lane == row + ROWS, sum_column, 0.0)),
-            0,
-            keepdims=True,
-        )
-
-    def joined(store, count):
-        highs = [to_rows(store[i], 0) for i in range(count)]
-        sums = [to_rows(store[i], ROWS) for i in range(count)]
-        peak = highs[0]
-        for item in highs[1:]:
-            peak = jnp.maximum(peak, item)
-        summed = sums[0] * jnp.exp(highs[0] - peak)
-        for i in range(1, count):
-            summed = summed + sums[i] * jnp.exp(highs[i] - peak)
-        return peak, summed
-
-    lsa_all[me_s] = packed(high_here, sum_here)
-    more = exchange(lambda peer: lsa_all.at[me_s], lsa_all, lsa_s, lsa_r, "seq")
-    for copy in more:
-        copy.wait_recv()
-    sent += more
-    lsb_all[me_t] = packed(*joined(lsa_all, n_seq))
-    more = exchange(lambda peer: lsb_all.at[me_t], lsb_all, lsb_s, lsb_r, "tensor")
-    for copy in more:
-        copy.wait_recv()
-    sent += more
-    peak, summed = joined(lsb_all, n_tensor)
-    answer = logits[...] - (peak + jnp.log(summed))
-    for b in range(streams):
-        logp_ref[b] = answer[2 * b : 2 * b + 2]
+    stores = []
+    highs = []
+    for h in range(HALVES):
+        i = (groups - 1) * HALVES + h
+        pair_copies[i].wait_recv()
+        value = own[i] + pair_in[i].astype(F32)
+        for k in range(1, groups):
+            far_copies[(k - 1) * HALVES + h].wait_recv()
+            value = value + far_in[(k - 1) * HALVES + h].astype(F32)
+        value = value * scale
+        logits[h] = value
+        store = pltpu.make_async_copy(
+            logits.at[h], logits_hbm.at[:, pl.ds(h * half, half)], dma_sem.at[8 + h]
+        )
+        store.start()
+        stores.append(store)
+        highs.append(jnp.max(value, -1, keepdims=True))
+    high_here = highs[0]
+    for item in highs[1:]:
+        high_here = jnp.maximum(high_here, item)
+    sum_here = jnp.zeros_like(high_here)
+    for h in range(HALVES):
+        sum_here = sum_here + jnp.sum(jnp.exp(logits[h] - high_here), -1, keepdims=True)
+
+    devices = n_seq * n_tensor
+    me = me_s * n_tensor + me_t
+    ls_all[me] = jnp.concatenate([to_lanes(high_here), to_lanes(sum_here)], 0)
+
+    def ls_copy(k):
+        peer = lax.rem(me + k, devices)
+        return pltpu.make_async_remote_copy(
+            src_ref=ls_all.at[me],
+            dst_ref=ls_all.at[me],
+            send_sem=ls_s.at[k],
+            recv_sem=ls_r.at[k],
+            device_id=(lax.div(peer, n_tensor), lax.rem(peer, n_tensor)),
+            device_id_type=pl.DeviceIdType.MESH,
+        )
+
+    def each(action):
+        def step_of(k, carry):
+            action(ls_copy(k))
+            return carry
+
+        lax.fori_loop(1, devices, step_of, 0)
+
+    each(lambda copy: copy.start())
     for copy in sent + pair_copies + sq_copies + far_copies:
         copy.wait_send()
+    each(lambda copy: copy.wait_recv())
+    peak = ls_all[0]
+    for i in range(1, devices):
+        peak = jnp.maximum(peak, ls_all[i])
+    peak = peak[0:1]
+    summed = jnp.zeros_like(peak)
+    for i in range(devices):
+        line = ls_all[i]
+        summed = summed + line[1:2] * jnp.exp(line[0:1] - peak)
+    lse_ref[...] = jnp.broadcast_to(to_rows(peak + jnp.log(summed), 0), (ROWS, HD))
+    each(lambda copy: copy.wait_send())
+    for store in stores:
+        store.wait()
+
+
+def close_kernel(streams, hidden_in, fresh_k, fresh_v, lse, logits, hidden_ref, newkv_ref, logp_ref):
+    hidden = hidden_in[...]
+    new_keys = fresh_k[...]
+    new_values = fresh_v[...]
+    answer = logits[...] - lse[:, :1]
+    for b in range(streams):
+        hidden_ref[b] = hidden[2 * b : 2 * b + 2]
+        newkv_ref[0, b] = new_keys[2 * b : 2 * b + 2]
+        newkv_ref[1, b] = new_values[2 * b : 2 * b + 2]
+        logp_ref[b] = answer[2 * b : 2 * b + 2]
 
 
 def body(
@@ -382,15 +423,17 @@
         compiler_params=pltpu.CompilerParams(vmem_limit_bytes=60 * 1024 * 1024),
         name="rows",
     )(token_ids, cache_lengths, freq, embed_table)
-    hidden, new_kv, logprobs = pl.pallas_call(
+    closing = pl.pallas_call(
         functools.partial(kernel, n_seq, n_tensor, streams, model_width),
         out_shape=(
-            jax.ShapeDtypeStruct((streams, 2, HD), BF),
-            jax.ShapeDtypeStruct((2, streams, 2, HD), BF),
-            jax.ShapeDtypeStruct((streams, 2, share), F32),
+            row_shape(BF),
+            row_shape(BF),
+            row_shape(BF),
+            row_shape(F32),
+            jax.ShapeDtypeStruct((ROWS, share), F32),
         ),
         in_specs=[vmem] * 6 + [hbm] * 5,
-        out_specs=(vmem, vmem, vmem),
+        out_specs=(vmem,) * 4 + (hbm,),
         scratch_shapes=[
             pltpu.VMEM((vocab_rows, HD), BF),
             pltpu.VMEM((3, model_width, HD), BF),
@@ -403,20 +446,19 @@
             pltpu.VMEM((n_tensor, ROWS, HD), F32),
             pltpu.VMEM((n_tensor, ROWS, HD), F32),
             pltpu.VMEM((n_tensor, 1, HD), F32),
-            pltpu.VMEM((n_seq, 1, HD), F32),
-            pltpu.VMEM((n_tensor, 1, HD), F32),
-            pltpu.VMEM((groups, ROWS, share), BF),
-            pltpu.VMEM((groups, ROWS, share), BF),
-            pltpu.VMEM((groups, ROWS, share), F32),
-            pltpu.VMEM((groups, ROWS, share), BF),
-            pltpu.VMEM((groups, ROWS, share), BF),
-            pltpu.VMEM((ROWS, share), F32),
-            sems(8),
+            pltpu.VMEM((n_seq * n_tensor, 2, HD), F32),
+            pltpu.VMEM((groups * HALVES, ROWS, share // HALVES), BF),
+            pltpu.VMEM((groups * HALVES, ROWS, share // HALVES), BF),
+            pltpu.VMEM((groups * HALVES, ROWS, share // HALVES), F32),
+            pltpu.VMEM((groups * HALVES, ROWS, share // HALVES), BF),
+            pltpu.VMEM((groups * HALVES, ROWS, share // HALVES), BF),
+            pltpu.VMEM((HALVES, ROWS, share // HALVES), F32),
+            sems(8 + HALVES),
             sems(n_seq), sems(n_seq), sems(n_tensor), sems(n_tensor),
             sems(n_seq), sems(n_seq), sems(n_tensor), sems(n_tensor),
             sems(n_tensor), sems(n_tensor),
-            sems(n_seq), sems(n_seq), sems(n_tensor), sems(n_tensor),
-            sems(groups), sems(groups), sems(groups), sems(groups),
+            sems(n_seq * n_tensor), sems(n_seq * n_tensor),
+            sems(groups * HALVES), sems(groups * HALVES), sems(groups * HALVES), sems(groups * HALVES),
         ],
         compiler_params=pltpu.CompilerParams(
             collective_id=0, has_side_effects=True, vmem_limit_bytes=60 * 1024 * 1024
@@ -435,6 +477,18 @@
         cache_keys,
         cache_values,
     )
+    hidden, new_kv, logprobs = pl.pallas_call(
+        functools.partial(close_kernel, streams),
+        out_shape=(
+            jax.ShapeDtypeStruct((streams, 2, HD), BF),
+            jax.ShapeDtypeStruct((2, streams, 2, HD), BF),
+            jax.ShapeDtypeStruct((streams, 2, share), F32),
+        ),
+        in_specs=[vmem] * 5,
+        out_specs=(vmem,) * 3,
+        compiler_params=pltpu.CompilerParams(vmem_limit_bytes=60 * 1024 * 1024),
+        name="close",
+    )(*closing)
     return (
         jnp.transpose(hidden, (1, 0, 2)),
         jnp.transpose(new_kv, (0, 2, 1, 3)),

time: 57 us -> 51.6 us (0.905)
  local copies, waits for them, and re-layouts: 4.2 us -> 0 us
  Pallas kernels: 51.8 us -> 50.7 us
    unnamed x3 -> x0, local copies, waits for them, and re-layouts: 4.2 us -> none
    pallas_call x1, Pallas kernels: 49.3 us -> 46.4 us  [body(): pl.pallas_call(functools.partial(kernel, n_seq, n_tensor, streams, model_...]
    pallas_call x0 -> x1, Pallas kernels: none -> 1.78 us  [body(): pl.pallas_call(functools.partial(close_kernel, streams), out_shape=(jax.S...]
where the time goes in v2:
time: 51.6 us; the launch traced here: 51.3 us
  Pallas kernels  50.7 us (98%)
  between operations  0.65 us (1%)
    pallas_call x1, Pallas kernels, body(): pl.pallas_call(functools.partial(kernel, n_seq, n_tensor, streams, model_...  46.4 us
    pallas_call x1, Pallas kernels, body(): pl.pallas_call(functools.partial(local_kernel, streams), out_shape=(row_s...  2.48 us
    pallas_call x1, Pallas kernels, body(): pl.pallas_call(functools.partial(close_kernel, streams), out_shape=(jax.S...  1.78 us

profile of v2, /device:TPU:0, one launch (start us, length us, event | category | flops | bytes accessed | tf_op | source)
XLA Modules:
  0.0 51.3 jit_solution(14988201604061763144)
XLA Ops:
  0.6 2.5 %rows.1 = (bf16[16,128]{1,0:T(8,128)(2,1)}, s32[16,128]{1,0:T(8,128)}, f32[16,128]{1,0:T(8,128)}, f32[16,128]{1,0:T(8,128)}) custom-call(s32[2,7]{1,0:T(2,128)} %tok_ref.1, s32[7]{0:T(128)} %len_ref.1, f32[1,128]{1,0:T(1,128)} %constant.2.clone.freq_ref, bf16[32768,128]{1,0:T(8,128)(2,1)} %table_hbm.3), custom_call_target="tpu_custom_call" | custom-call | tf_op jit(solution)/shard_map/rows/pallas_call | solution.py:417
  3.1 46.4 %decode.1 = (bf16[16,128]{1,0:T(8,128)(2,1)}, bf16[16,128]{1,0:T(8,128)(2,1)}, bf16[16,128]{1,0:T(8,128)(2,1)}, f32[16,128]{1,0:T(8,128)}, f32[16,4096]{1,0:T(8,128)}) custom-call(bf16[16,128]{1,0:T(8,128)(2,1)} %get-tuple-element.15.pick_ref, s32[16,128]{1,0:T(8,128)} %get-tuple-element.16.lens_ref, f32[16,128]{1,0:T(8,128)} %get-tuple-element.17.cos_ref, ...), custom_call_target="tpu_custom_call" | custom-call | tf_op jit(solution)/shard_map/decode/pallas_call | solution.py:426
  49.5 1.8 %close.1 = (bf16[7,2,128]{2,1,0:T(2,128)(2,1)}, bf16[2,7,2,128]{3,2,1,0:T(2,128)(2,1)}, f32[7,2,4096]{2,1,0:T(2,128)}) custom-call(bf16[16,128]{1,0:T(8,128)(2,1)} %get-tuple-element.19.hidden_in, bf16[16,128]{1,0:T(8,128)(2,1)} %get-tuple-element.20.fresh_k, bf16[16,128]{1,0:T(8,128)(2,1)} %get-tuple-element.21.fresh_v, f32[16,128]{1,0:T(8,128)} %get-tuple-element.22.lse, ...), custom_call_target="tpu_custom_call" | custom-call | tf_op jit(solution)/shard_map/close/pallas_call | solution.py:480

commit v3 on v2

--- a/solution.py
+++ b/solution.py
@@ -25,46 +25,9 @@
     return lax.dot_general(a, b, (((1,), (1,)), ((), ())), preferred_element_type=F32)
 
 
-def local_kernel(streams, tok_ref, len_ref, freq_ref, table_hbm, pick_ref, lens_ref, cos_ref, sin_ref, blocks, sem):
-    first = lax.axis_index("seq") * table_hbm.shape[0]
-    last = table_hbm.shape[0] - 1
-    lines = []
-    copies = []
-    for b in range(streams):
-        for s in range(2):
-            at = tok_ref[s, b] - first
-            inside = (at >= 0) & (at <= last)
-            safe = jnp.clip(at, 0, last)
-            base = lax.div(safe, TILE) * TILE
-            copy = pltpu.make_async_copy(
-                table_hbm.at[pl.ds(pl.multiple_of(base, TILE), TILE)],
-                blocks.at[2 * b + s],
-                sem.at[2 * b + s],
-            )
-            copy.start()
-            copies.append(copy)
-            lines.append(jnp.where(inside, safe - base, -1))
-    row = lax.broadcasted_iota(jnp.int32, (ROWS, HD), 0)
-    lane = lax.broadcasted_iota(jnp.int32, (ROWS, HD), 1)
-    lens = jnp.ones((ROWS, HD), jnp.int32)
-    for b in range(streams):
-        lens = jnp.where(lax.div(row, 2) == b, len_ref[b], lens)
-    lens_ref[...] = lens
-    angle = (lens + lax.rem(row, 2)).astype(F32) * freq_ref[...]
-    cos_ref[...] = jnp.cos(angle)
-    sine = jnp.sin(angle)
-    sin_ref[...] = jnp.where(lane < HD // 2, -sine, sine)
-    picked = jnp.zeros((ROWS, HD), F32)
-    for i in range(2 * streams):
-        copies[i].wait()
-        line = jnp.where(row == lines[i], blocks[i].astype(F32), 0.0)
-        picked = jnp.where(row == i, jnp.sum(line, 0, keepdims=True), picked)
-    pick_ref[...] = picked.astype(BF)
-
-
 def kernel(
     n_seq, n_tensor, streams, model_width,
-    pick_ref, lens_ref, cos_ref, sin_ref, again_ref, fgain_ref, table_hbm, wqkv_hbm, wout_hbm, keys_hbm, values_hbm,
+    tok_ref, len_ref, freq_ref, again_ref, fgain_ref, table_hbm, wqkv_hbm, wout_hbm, keys_hbm, values_hbm,
     hidden_ref, fresh_k_ref, fresh_v_ref, lse_ref, logits_hbm,
     table, wqkv, wout, keys, values,
     pick_all, emb_all, flash_all, mix_out, mix_all, sq_all, ls_all,
@@ -75,13 +38,14 @@
 ):
     me_s = lax.axis_index("seq")
     me_t = lax.axis_index("tensor")
-    vocab_rows = table.shape[0]
+    tiles = table.shape[0]
+    vocab_rows = tiles * TILE
     slot_count = keys.shape[1]
     groups = n_tensor // 2
     share = vocab_rows // n_tensor
 
     parts = 4
-    piece = vocab_rows // parts
+    piece = tiles // parts
     loads = [
         pltpu.make_async_copy(
             table_hbm.at[pl.ds(i * piece, piece)], table.at[pl.ds(i * piece, piece)], dma_sem.at[i]
@@ -138,12 +102,25 @@
     lane = lax.broadcasted_iota(jnp.int32, (ROWS, HD), 1)
     stream = lax.div(row, 2)
     step = lax.rem(row, 2)
-    lens = lens_ref[...]
-    cosine = cos_ref[...]
-    sine = sin_ref[...]
-    pick_all[me_s] = pick_ref[...]
+    lens = jnp.ones((ROWS, HD), jnp.int32)
+    for b in range(streams):
+        lens = jnp.where(stream == b, len_ref[b], lens)
+    angle = (lens + step).astype(F32) * freq_ref[...]
+    cosine = jnp.cos(angle)
+    sine = jnp.sin(angle)
+    sine = jnp.where(lane < HD // 2, -sine, sine)
+    for load in loads:
+        load.wait()
+    picked = jnp.zeros((ROWS, HD), F32)
+    for b in range(streams):
+        for s in range(2):
+            at = tok_ref[s, b] - me_s * vocab_rows
+            tile = lax.div(jnp.minimum(jnp.maximum(at, 0), vocab_rows - 1), TILE)
+            line = jnp.where(row == at - tile * TILE, table[tile].astype(F32), 0.0)
+            picked = jnp.where(row == 2 * b + s, jnp.sum(line, 0, keepdims=True), picked)
+    pick_all[me_s] = picked.astype(BF)
     pl.semaphore_wait(barrier, n_seq - 1 + n_tensor - 1)
-    sent = exchange(lambda peer: pick_ref, pick_all, pick_s, pick_r, "seq")
+    sent = exchange(lambda peer: pick_all.at[me_s], pick_all, pick_s, pick_r, "seq")
     for copy in sent:
         copy.wait_recv()
     embed = pick_all[0].astype(F32)
@@ -152,8 +129,6 @@
     emb_all[me_t] = embed.astype(BF)
     more = exchange(lambda peer: emb_all.at[me_t], emb_all, emb_s, emb_r, "tensor")
     load_wqkv.wait()
-    for load in loads:
-        load.wait()
     for copy in more:
         copy.wait_recv()
     sent += more
@@ -265,8 +240,8 @@
     half = share // HALVES
 
     def part_logits(owner, h):
-        start = pl.multiple_of(owner * share + h * half, half)
-        return nt_dot(gated, table[pl.ds(start, half), :])
+        start = owner * (share // TILE) + h * (half // TILE)
+        return nt_dot(gated, table[pl.ds(start, half // TILE)].reshape(half, HD))
 
     pair_copies = []
     for k in range(1, groups + 1):
@@ -414,15 +389,6 @@
     hbm = pl.BlockSpec(memory_space=pl.ANY)
     sems = lambda n: pltpu.SemaphoreType.DMA((n,))
     row_shape = lambda dtype: jax.ShapeDtypeStruct((ROWS, HD), dtype)
-    picked, lens, cosine, sine = pl.pallas_call(
-        functools.partial(local_kernel, streams),
-        out_shape=(row_shape(BF), row_shape(jnp.int32), row_shape(F32), row_shape(F32)),
-        in_specs=[smem, smem, vmem, hbm],
-        out_specs=(vmem,) * 4,
-        scratch_shapes=[pltpu.VMEM((2 * streams, TILE, HD), BF), sems(2 * streams)],
-        compiler_params=pltpu.CompilerParams(vmem_limit_bytes=60 * 1024 * 1024),
-        name="rows",
-    )(token_ids, cache_lengths, freq, embed_table)
     closing = pl.pallas_call(
         functools.partial(kernel, n_seq, n_tensor, streams, model_width),
         out_shape=(
@@ -432,10 +398,10 @@
             row_shape(F32),
             jax.ShapeDtypeStruct((ROWS, share), F32),
         ),
-        in_specs=[vmem] * 6 + [hbm] * 5,
+        in_specs=[smem, smem, vmem, vmem, vmem] + [hbm] * 5,
         out_specs=(vmem,) * 4 + (hbm,),
         scratch_shapes=[
-            pltpu.VMEM((vocab_rows, HD), BF),
+            pltpu.VMEM((vocab_rows // TILE, TILE, HD), BF),
             pltpu.VMEM((3, model_width, HD), BF),
             pltpu.VMEM((HD, model_width), BF),
             pltpu.VMEM((streams, slot_count, HD), BF),
@@ -465,13 +431,12 @@
         ),
         name="decode",
     )(
-        picked,
-        lens,
-        cosine,
-        sine,
+        token_ids,
+        cache_lengths,
+        freq,
         attn_gain.reshape(1, model_width),
         final_gain.reshape(n_tensor, 1, HD),
-        embed_table,
+        embed_table.reshape(vocab_rows // TILE, TILE, HD),
         jnp.transpose(w_qkv, (1, 0, 2)),
         w_out,
         cache_keys,

time: 51.6 us -> 49.6 us (0.961)
  Pallas kernels: 50.7 us -> 48.8 us
    pallas_call x1 -> x0, Pallas kernels: 2.48 us -> none  [body(): pl.pallas_call(functools.partial(local_kernel, streams), out_shape=(row_s...]
    pallas_call x1, Pallas kernels: 46.4 us -> 47 us  [body(): pl.pallas_call(functools.partial(kernel, n_seq, n_tensor, streams, model_...]
where the time goes in v3:
time: 49.6 us; the launch traced here: 49.5 us
  Pallas kernels  48.8 us (98%)
  between operations  0.64 us (1%)
    pallas_call x1, Pallas kernels, body(): pl.pallas_call(functools.partial(kernel, n_seq, n_tensor, streams, model_...  47 us
    pallas_call x1, Pallas kernels, body(): pl.pallas_call(functools.partial(close_kernel, streams), out_shape=(jax.S...  1.78 us

profile of v3, /device:TPU:0, one launch (start us, length us, event | category | flops | bytes accessed | tf_op | source)
XLA Modules:
  0.0 49.5 jit_solution(17816701508786699477)
XLA Ops:
  0.6 47.0 %decode.1 = (bf16[16,128]{1,0:T(8,128)(2,1)}, bf16[16,128]{1,0:T(8,128)(2,1)}, bf16[16,128]{1,0:T(8,128)(2,1)}, f32[16,128]{1,0:T(8,128)}, f32[16,4096]{1,0:T(8,128)}) custom-call(s32[2,7]{1,0:T(2,128)} %tok_ref.1, s32[7]{0:T(128)} %len_ref.1, f32[1,128]{1,0:T(1,128)} %constant.2.clone.freq_ref, f32[1,1024]{1,0:T(1,128)} %bitcast.9, f32[8,1,128]{2,1,0:T(1,128)} %bitcast.10, ...), custom_call_target="tpu_custom_call" | custom-call | tf_op jit(solution)/shard_map/decode/pallas_call | solution.py:392
  47.7 1.8 %close.1 = (bf16[7,2,128]{2,1,0:T(2,128)(2,1)}, bf16[2,7,2,128]{3,2,1,0:T(2,128)(2,1)}, f32[7,2,4096]{2,1,0:T(2,128)}) custom-call(bf16[16,128]{1,0:T(8,128)(2,1)} %get-tuple-element.11.hidden_in, bf16[16,128]{1,0:T(8,128)(2,1)} %get-tuple-element.12.fresh_k, bf16[16,128]{1,0:T(8,128)(2,1)} %get-tuple-element.13.fresh_v, f32[16,128]{1,0:T(8,128)} %get-tuple-element.14.lse, ...), custom_call_target="tpu_custom_call" | custom-call | tf_op jit(solution)/shard_map/close/pallas_call | solution.py:445
